TPU v7x, 512 devices: a whole 4x4x16 slice. The times are simulated.
512 devices in a mesh: rows: 128 (over x, z, core), rep: 4 (over y).
Axes of the slice: x: 4, y: 4, z: 16, core: 2. Of those that a mesh axis runs over, the one named last changes fastest.
Arguments:
- requests: int32 [512, 128, 8], P(('rows', 'rep')), may hold values from 0 to 1023
- request_counts: int32 [512, 128], P(('rows', 'rep')), may hold values from 0 to 8, as said below
- table: bfloat16 [131072, 512], P('rows')
- gain: float32 [512], replicated, may hold values from 0.5 to 1.5
Outputs:
- normalized: bfloat16 [512, 128, 8, 512], P(('rows', 'rep'))
- row_counts: int32 [131072], P('rows')
- moments: float32 [2, 2], replicated
Inputs may be any that keep to these rules, and one draw needn't show every extreme that they name: Each device uses request_counts[d, o] of its 8 slots toward owner o; in every draw one owner's slots are full from every device.
All inputs are finite; a program needn't handle non-finite values.
Results may differ from a plain program's by a relative error of at most 0.0004.
Values may be sent and summed in bfloat16 or wider, within the bound.
A program may use at most 64 MiB of HBM per device.

v0:
```python
import math

import jax
import jax.numpy as jnp
from jax import lax
from jax.sharding import Mesh
from jax.sharding import PartitionSpec as P

WIDTH = 256
LAYERS = 2
ROWS = ("rows_0", "rows_1", "rows_2")
ROWS_REP = ("rows_0", "rows_1", "rows_2", "rep")


epsilon = 1e-06


def sent_together(arrays, axis, split_dim, concat_dim, along):
    widths = [math.prod(a.shape[along:]) for a in arrays]
    both = jnp.concatenate(
        [a.reshape(*a.shape[:along], w) for a, w in zip(arrays, widths)], axis=along
    )
    filled = lax.all_to_all(both, axis, split_axis=split_dim, concat_axis=concat_dim, tiled=True)
    pieces = jnp.split(filled, [sum(widths[:k]) for k in range(1, len(widths))], axis=along)
    return tuple(
        (b.reshape(*filled.shape[:along], *a.shape[along:]) for a, b in zip(arrays, pieces))
    )


def sent_to_all(value, axis):
    count = lax.axis_size(axis)
    return lax.all_to_all(
        jnp.broadcast_to(value[None], (count, *value.shape)), axis, 0, 0, tiled=True
    )


def taken_together(value, axis):
    everything = sent_to_all(value, axis)
    return jnp.sum(everything, axis=0)


def collected_together(value, axis):
    leaves = jax.tree.leaves(value)
    sequence = sorted(range(len(leaves)), key=lambda k: -leaves[k].size)
    width = (1, *leaves[sequence[0]].shape)[-1]
    lines = [
        jnp.pad(leaves[k].reshape(-1), (0, -leaves[k].size % width)).reshape(-1, width)
        for k in sequence
    ]
    both, at, found = (lax.all_gather(jnp.concatenate(lines), axis), 0, {})
    for k, line in zip(sequence, lines):
        slab = both[:, at : at + len(line)].reshape(len(both), -1)
        found[k] = slab[:, : leaves[k].size].reshape(-1, *leaves[k].shape)
        at += len(line)
    numbers = iter(range(len(leaves)))
    return jax.tree.map(lambda _: found[next(numbers)], value)


def joined_all(value, axes, combine):
    for axis in axes:
        pieces = collected_together(value, axis)
        value = jax.tree.map(lambda part: part[0], pieces)
        for k in range(1, lax.axis_size(axis)):
            value = combine(value, jax.tree.map(lambda part: part[k], pieces))
    return value


def merge_moments(former, latter):
    count_former, mean_former, square_former = former
    count_latter, mean_latter, square_latter = latter
    merged_count = count_former + count_latter
    safe_count = jnp.maximum(merged_count, 1.0)
    delta_mean = mean_latter - mean_former
    merged_mean = mean_former + delta_mean * count_latter / safe_count
    merged_square = (
        square_former
        + square_latter
        + delta_mean * delta_mean * count_former * count_latter / safe_count
    )
    return (merged_count, merged_mean, merged_square)


def per_device(requests, request_counts, table, gain):
    wanted, wanted_counts = sent_together((requests, request_counts), ROWS, 1, 0, 2)
    owners = wanted.shape[0]
    slot_count = wanted.shape[2]
    held_rows = table.shape[0]
    row_index = wanted.reshape(-1)
    live_slot = lax.broadcasted_iota(jnp.int32, (owners, slot_count), 1) < wanted_counts
    live_flat = live_slot.reshape(-1)
    matches = (row_index[:, None] == jnp.arange(held_rows, dtype=jnp.int32)[None, :]) & live_flat[
        :, None
    ]
    local_counts = jnp.sum(matches.astype(jnp.int32), axis=0)
    row_counts = taken_together(local_counts, "rep")
    shaped = table.reshape(held_rows, LAYERS, WIDTH)
    weights = row_counts.astype(jnp.float32)
    partial_value = jnp.dot(
        weights, jnp.sum(shaped, axis=2, dtype=jnp.float32), precision=lax.Precision.HIGHEST
    )
    count_layers = jnp.full((LAYERS,), jnp.sum(weights) * WIDTH, jnp.float32)
    mean_here = partial_value / jnp.maximum(count_layers, 1.0)
    centered = jnp.sum(jnp.square(shaped.astype(jnp.float32) - mean_here[None, :, None]), axis=2)
    square_here = jnp.dot(weights, centered, precision=lax.Precision.HIGHEST)
    entries, layer_mean, merged_square = joined_all(
        (count_layers, mean_here, square_here), ROWS, merge_moments
    )
    layer_var = merged_square / entries
    inverse = jnp.repeat(lax.rsqrt(layer_var + epsilon), WIDTH) * gain
    mean_full = jnp.repeat(layer_mean, WIDTH)
    looked = jnp.take(table, row_index, axis=0).reshape(owners, 1, slot_count, LAYERS * WIDTH)
    finished = (
        lax.all_to_all(looked, ROWS, split_axis=0, concat_axis=1, tiled=True).astype(jnp.float32)
        - mean_full
    ) * inverse
    own_live = (
        lax.broadcasted_iota(jnp.int32, request_counts.shape + (slot_count,), 2)
        < request_counts[:, :, None]
    )
    normalized = jnp.where(own_live[..., None], finished, 0.0).astype(jnp.bfloat16)
    return (normalized, row_counts, jnp.stack([layer_mean, layer_var]))


def solution(mesh):
    finer = Mesh(
        mesh.devices.reshape(4, 16, 2, mesh.shape["rep"]), ("rows_0", "rows_1", "rows_2", "rep")
    )
    placed = (P(ROWS_REP, None, None), P(ROWS_REP, None), P(ROWS, None), P())
    return jax.shard_map(
        per_device,
        mesh=finer,
        in_specs=placed,
        out_specs=(P(ROWS_REP, None, None, None), P(ROWS), P()),
        check_vma=False,
    )
```

profile of v0, /device:TPU:1, one launch (start us, length us, event | category | flops | bytes accessed | tf_op | source)
XLA Modules:
  0.0 134.3 jit_solution(5812315129534532759)
XLA Ops:
  0.6 0.7 pad_add_fusion
  1.3 0.1 copy.39
  1.5 35.2 %all_to_all.27 = s32[1,128,9]{2,0,1:T(1,128)S(1)} all-to-all(s32[1,128,9]{2,0,1:T(1,128)S(1)} %copy.39), channel_id=1, replica_groups=mesh['rows_0'=4,'rows_1'=16,'rows_2'=2,'rep'=4] {'rows_0','rows_1','rows..., dimensions={1} | all-to-all | bytes 9216 | tf_op jit(solution)/shard_map/all_to_all | solution.py:23
  36.7 0.2 slice_reduce_fusion
  36.9 0.1 reshape.2049
  37.0 0.1 reshape.2048
  37.2 0.1 lt.65
  37.3 0.8 convert_reduce_fusion
  38.1 0.6 broadcast_in_dim.48
  38.7 4.2 %all-to-all-start.2 = ((s32[4,1,1024]{2,1,0:T(1,128)}), s32[4,1,1024]{2,1,0:T(1,128)S(1)}, u32[]{:S(2)}, u32[]{:S(2)}) async-start(s32[4,1,1024]{2,1,0:T(1,128)} %broadcast_in_dim.48), calls=%async_computation.2 | async-start | bytes 32768 | tf_op jit(solution)/shard_map/all_to_all | solution.py:32
  42.9 5.4 %gather_fusion = bf16[1024,512]{1,0:T(8,128)(2,1)S(1)} fusion(bf16[1024,512]{1,0:T(8,128)(2,1)} %param.6, s32[1024]{0:T(1024)S(1)} %broadcast_clamp_fusion), kind=kCustom, calls=%fused_computation | custom fusion | bytes 2101248 | tf_op jit(solution)/shard_map/jit(_take)/gather | solution.py:111
  48.3 1.2 bitcast_select_fusion
  49.4 7.9 %all-to-all-start.1 = ((bf16[128,1,8,512]{3,2,1,0:T(8,128)(2,1)}), bf16[128,1,8,512]{3,2,1,0:T(8,128)(2,1)}, u32[]{:S(2)}, u32[]{:S(2)}) async-start(bf16[128,1,8,512]{3,2,1,0:T(8,128)(2,1)} %bitcast_select_fusion), calls=%async_computation.1 | async-start | bytes 2097152 | tf_op jit(solution)/shard_map/all_to_all | solution.py:113
  57.4 1.3 reshape.2055
  58.7 1.2 reduce_sum.48
  60.1 0.6 convert_reduce_fusion.1
  61.3 0.4 fusion.4
  61.7 1.3 multiply_reduce_fusion
  62.9 0.4 fusion.81
  63.4 0.1 copy.42
  63.5 9.3 %all-gather.3 = f32[4,3,2]{1,2,0:T(2,128)S(1)} all-gather(f32[1,3,2]{1,2,0:T(2,128)S(1)} %bitcast.1026), channel_id=2, replica_groups=mesh['rows_0'=4,'rows_1'=16,'rows_2'=2,'rep'=4] {'rows_0'}, dimensions={0}, use_global_device_ids=true | all-gather | bytes 120 | tf_op jit(solution)/shard_map/all_gather | solution.py:50
  72.7 0.4 slice_reduce_fusion.55
  73.3 48.4 %all-gather.4 = f32[16,3,2]{1,2,0:T(2,128)S(1)} all-gather(f32[1,3,2]{1,2,0:T(2,128)S(1)} %bitcast.1027), channel_id=3, replica_groups=mesh['rows_0'=4,'rows_1'=16,'rows_2'=2,'rep'=4] {'rows_1'}, dimensions={0}, use_global_device_ids=true | all-gather | bytes 408 | tf_op jit(solution)/shard_map/all_gather | solution.py:50
  121.7 0.3 slice_reduce_fusion.50
  121.9 0.5 slice_reduce_fusion.23
  122.4 0.5 slice_reduce_fusion.19
  123.0 0.1 fusion.79
  123.1 0.1 copy.44
  123.2 7.6 %all-gather.5 = f32[2,3,2]{1,2,0:T(2,128)S(1)} all-gather(f32[1,3,2]{1,2,0:T(2,128)S(1)} %bitcast.1028), channel_id=4, replica_groups=mesh['rows_0'=4,'rows_1'=16,'rows_2'=2,'rep'=4] {'rows_2'}, dimensions={0}, use_global_device_ids=true | all-gather | bytes 72 | tf_op jit(solution)/shard_map/all_gather | solution.py:50
  130.8 0.2 slice_reduce_fusion.4
  131.2 0.6 pad_maximum_fusion.3
  131.8 2.6 %fusion.3 = bf16[1,128,8,512]{3,2,1,0:T(8,128)(2,1)} fusion(bf16[128,1,8,512]{3,2,1,0:T(8,128)(2,1)} %all-to-all-done.1, f32[512]{0:T(512)S(1)} %mul.931, f32[512]{0:T(512)S(1)} %bitcast.1024, pred[128,8]{1,0:T(8,128)(4,1)S(1)} %iota_compare_fusion.2), kind=kLoop, calls=%fused_computation.7 | loop fusion | flops 2621440 | bytes 2102272 | tf_op jit(solution)/shard_map/convert_element_type | solution.py:120
  (31 shorter events, 0.7 us)
Async XLA Ops:
  38.7 10.8 %all-to-all-start.2 = ((s32[4,1,1024]{2,1,0:T(1,128)}), s32[4,1,1024]{2,1,0:T(1,128)S(1)}, u32[]{:S(2)}, u32[]{:S(2)}) async-start(s32[4,1,1024]{2,1,0:T(1,128)} %broadcast_in_dim.48), calls=%async_computation.2 | async-start | bytes 32768 | tf_op jit(solution)/shard_map/all_to_all | solution.py:32
  48.2 9.1 %copy-start = (bf16[1024,512]{1,0:T(8,128)(2,1)S(1)}, bf16[1024,512]{1,0:T(8,128)(2,1)}, u32[]{:S(2)}) copy-start(bf16[1024,512]{1,0:T(8,128)(2,1)} %param.6) | copy-start | bytes 3145732
  49.4 82.3 %all-to-all-start.1 = ((bf16[128,1,8,512]{3,2,1,0:T(8,128)(2,1)}), bf16[128,1,8,512]{3,2,1,0:T(8,128)(2,1)}, u32[]{:S(2)}, u32[]{:S(2)}) async-start(bf16[128,1,8,512]{3,2,1,0:T(8,128)(2,1)} %bitcast_select_fusion), calls=%async_computation.1 | async-start | bytes 2097152 | tf_op jit(solution)/shard_map/all_to_all | solution.py:113
  58.7 1.2 copy-start.3
  59.9 71.3 %copy-start.2 = (f32[512]{0:T(512)S(1)}, f32[512]{0:T(512)}, u32[]{:S(2)}) copy-start(f32[512]{0:T(512)} %param.7) | copy-start | bytes 6148
  60.0 74.3 %copy-start.1 = (s32[1024]{0:T(1024)}, s32[1024]{0:T(1024)S(1)}, u32[]{:S(2)}) copy-start(s32[1024]{0:T(1024)S(1)} %reduce_sum.46) | copy-start | bytes 12292
where the time goes:
time: 135 us; the launch traced here: 134 us
  blocking collectives  101 us (75%)
  starting transfers between devices  12.1 us (9%)
  other arithmetic  10.5 us (8%)
  local copies, waits for them, and re-layouts  9.04 us (7%)
  between operations  1.49 us (1%)
    all_gather x3, blocking collectives, collected_together(): both, at, found = (lax.all_gather(jnp.concatenate(lines), axis), 0, {})  65.3 us
    all_to_all x1, blocking collectives, sent_together(): lax.all_to_all(both, axis, split_axis=split_dim, concat_axis=concat_dim,...  35.2 us
    all_to_all x1, starting transfers between devices, per_device(): lax.all_to_all(looked, ROWS, split_axis=0, concat_axis=1, tiled=True)  7.93 us
    gather x1, local copies, waits for them, and re-layouts, per_device(): jnp.take(table, row_index, axis=0)  5.35 us
    all_to_all x1, starting transfers between devices, sent_to_all(): lax.all_to_all(jnp.broadcast_to(value[None], (count, *value.shape)), axis...  4.18 us
  transfers between devices with their start and end apart: 2, of which 0 were waited for; matrix products, arithmetic and copies ran while one was open for 11% of the time, Pallas kernels for 0%

commit v1 on v0

v1 whole, which is shorter than its diff:
```python
import functools

import jax
import jax.numpy as jnp
from jax import lax
from jax.experimental import pallas as pl
from jax.experimental.pallas import tpu as pltpu
from jax.sharding import Mesh
from jax.sharding import PartitionSpec as P

WIDTH = 256
LAYERS = 2
LANES = 128
ROWS = ("rows_0", "rows_1", "rows_2")
ROWS_REP = ("rows_0", "rows_1", "rows_2", "rep")
MESH = pl.DeviceIdType.MESH

epsilon = 1e-06


def merged(parts, lane):
    def pick(at):
        found = jnp.sum(jnp.where(lane == at, parts, 0.0), axis=2, keepdims=True)
        return jnp.broadcast_to(found, parts.shape)

    def over(value):
        return jnp.sum(value, axis=0, keepdims=True)

    line = lane[:1]
    each = pick(0)
    entries = over(each)
    row = jnp.where(line == 0, entries, 0.0)
    for layer in range(LAYERS):
        mean_each = pick(1 + layer)
        mean = over(each * mean_each) / jnp.maximum(entries, 1.0)
        gap = mean_each - mean
        square = over(pick(1 + LAYERS + layer) + each * gap * gap)
        row = jnp.where(line == 1 + layer, mean, row)
        row = jnp.where(line == 1 + LAYERS + layer, square, row)
    return row


def exchange(
    sizes,
    slots,
    ids_ref,
    table_ref,
    rows_ref,
    counts_ref,
    moments_ref,
    table,
    heard,
    asked,
    column,
    packed,
    passing,
    totals,
    tally,
    tally_all,
    own_row,
    side_row,
    plane_row,
    parts_rep,
    parts_side,
    parts_ring,
    local_sem,
    ids_send,
    ids_recv,
    ids_keep,
    ask_send,
    ask_recv,
    row_send,
    row_recv,
    out_send,
    out_recv,
    out_keep,
    tally_send,
    tally_recv,
    rep_send,
    rep_recv,
    side_send,
    side_recv,
    ring_send,
    ring_recv,
):
    count_x, count_z, count_c, count_y = sizes
    count_s = count_x * count_c
    held = table.shape[0]
    width = table.shape[1]
    x = lax.axis_index("rows_0")
    z = lax.axis_index("rows_1")
    c = lax.axis_index("rows_2")
    y = lax.axis_index("rep")
    side = x * count_c + c

    def on_ring(at):
        return {"rows_1": at}

    def on_side(at):
        return {"rows_0": lax.div(at, count_c), "rows_2": lax.rem(at, count_c)}

    def on_rep(at):
        return {"rep": at}

    ring_peers = [lax.rem(z + k, count_z) for k in range(1, count_z)]
    side_peers = [lax.rem(side + k, count_s) for k in range(1, count_s)]
    rep_peers = [lax.rem(y + k, count_y) for k in range(1, count_y)]

    def plane(step):
        far = lax.div(step + 1, 2)
        toward = 2 * lax.rem(step, 2) - 1
        return lax.rem(z + far * toward + count_z, count_z)

    load_table = pltpu.make_async_copy(table_ref, table, local_sem.at[0])
    load_table.start()
    load_ids = pltpu.make_async_copy(ids_ref.at[z], heard.at[z], local_sem.at[1])
    load_ids.start()

    barrier = pltpu.get_barrier_semaphore()
    for peer in ring_peers:
        pl.semaphore_signal(barrier, inc=1, device_id=on_ring(peer), device_id_type=MESH)
    for peer in side_peers:
        pl.semaphore_signal(barrier, inc=1, device_id=on_side(peer), device_id_type=MESH)
    for peer in rep_peers:
        pl.semaphore_signal(barrier, inc=1, device_id=on_rep(peer), device_id_type=MESH)
    pl.semaphore_wait(barrier, len(ring_peers) + len(side_peers) + len(rep_peers))

    def ids_copy(at):
        return pltpu.make_async_remote_copy(
            src_ref=ids_ref.at[at],
            dst_ref=heard.at[z],
            send_sem=ids_send.at[at],
            recv_sem=ids_recv.at[z],
            device_id=on_ring(at),
            device_id_type=MESH,
        )

    def ids_arrive(at):
        pltpu.make_async_copy(heard.at[at], heard.at[at], ids_recv.at[at]).wait()

    def start_ids(step, carry):
        ids_copy(plane(step)).start()
        return carry

    lax.fori_loop(1, count_z, start_ids, 0)

    def keep_copy(at):
        return pltpu.make_async_copy(heard.at[at], asked.at[at, side], ids_keep.at[at])

    def tell(at):
        keep_copy(at).start()
        for peer in side_peers:
            pltpu.make_async_remote_copy(
                src_ref=heard.at[at],
                dst_ref=asked.at[at, side],
                send_sem=ask_send.at[at],
                recv_sem=ask_recv.at[at],
                device_id=on_side(peer),
                device_id_type=MESH,
            ).start()

    def hear(step, carry=0):
        at = plane(step)
        ids_arrive(at)
        tell(at)
        return carry

    totals[...] = jnp.zeros_like(totals)
    tally[...] = jnp.zeros_like(tally)

    def look(step, carry=0):
        at = plane(step)
        keep_copy(at).wait()
        several = asked.at[at, pl.ds(0, count_s - 1)]
        pltpu.make_async_copy(several, several, ask_recv.at[at]).wait()
        shape = (count_s, slots, LANES)
        ids = jnp.broadcast_to(asked[at].astype(jnp.float32), shape)
        mine = lax.broadcasted_iota(jnp.int32, shape, 2) == side * slots + lax.broadcasted_iota(
            jnp.int32, shape, 1
        )
        wanted = jnp.sum(jnp.where(mine, ids, 0.0), axis=2, keepdims=True)
        wanted = jnp.broadcast_to(wanted, shape).reshape(count_s * slots, LANES)
        column[at] = wanted
        row_of = lax.broadcasted_iota(jnp.int32, wanted.shape, 1).astype(jnp.float32)
        hot = jnp.concatenate(
            [
                jnp.where(wanted == row_of + float(first), 1.0, 0.0).astype(jnp.bfloat16)
                for first in range(0, held, LANES)
            ],
            axis=1,
        )
        found = jnp.dot(hot, table[...], preferred_element_type=jnp.float32)
        found = found.reshape(count_s, slots, width)
        packed[at] = found.astype(jnp.bfloat16)
        totals[...] += jnp.sum(found, axis=0)
        ones = jnp.ones((8, count_s * slots), jnp.bfloat16)
        tally[...] += jnp.dot(ones, hot, preferred_element_type=jnp.float32)
        return carry

    def row_copy(at):
        return pltpu.make_async_remote_copy(
            src_ref=packed.at[at],
            dst_ref=passing.at[z],
            send_sem=row_send.at[at],
            recv_sem=row_recv.at[z],
            device_id=on_ring(at),
            device_id_type=MESH,
        )

    held_back = min(3, count_z - 1)

    def give(step):
        @pl.when(step >= held_back)
        def _():
            row_copy(plane(step)).start()

    ahead = min(5, count_z - 2)
    load_ids.wait()
    tell(z)
    lax.fori_loop(1, ahead + 1, hear, 0)
    load_table.wait()

    def both(step, carry):
        look(step)
        hear(step + ahead + 1)
        give(step - 1)
        return carry

    def only(step, carry):
        look(step)
        give(step - 1)
        return carry

    lax.fori_loop(0, count_z - 1 - ahead, both, 0)
    lax.fori_loop(count_z - 1 - ahead, count_z, only, 0)

    tally_all[y] = tally[0:1].astype(jnp.int32)
    entries = jnp.sum(tally[0:1], axis=1, keepdims=True) * float(WIDTH)
    summed = jnp.sum(totals[...], axis=0, keepdims=True)
    means = [
        jnp.sum(summed[:, layer * WIDTH : (layer + 1) * WIDTH], axis=1, keepdims=True)
        / jnp.maximum(entries, 1.0)
        for layer in range(LAYERS)
    ]
    center = jnp.concatenate([jnp.broadcast_to(m, (1, WIDTH)) for m in means], axis=1)
    give(count_z - 1)

    def squares(at, total):
        used = column[at] >= 0.0
        used = jnp.concatenate([used.astype(jnp.float32)] * (width // LANES), axis=1)
        used = used.reshape(count_s, slots, width)
        away = (packed[at].astype(jnp.float32) - center[None]) * used
        return total + jnp.sum(away * away, axis=0)

    spread = lax.fori_loop(0, count_z, squares, jnp.zeros((slots, width), jnp.float32))
    spread = jnp.sum(spread, axis=0, keepdims=True)
    lane = lax.broadcasted_iota(jnp.int32, (1, LANES), 1)
    row = jnp.where(lane == 0, entries, 0.0)
    for layer in range(LAYERS):
        square = jnp.sum(spread[:, layer * WIDTH : (layer + 1) * WIDTH], axis=1, keepdims=True)
        row = jnp.where(lane == 1 + layer, means[layer], row)
        row = jnp.where(lane == 1 + LAYERS + layer, square, row)
    own_row[...] = row[None]
    parts_rep[y] = row

    def out_row(at):
        return (x * count_z + at) * count_c + c

    def out_keep_copy(at):
        return pltpu.make_async_copy(
            passing.at[at, side], rows_ref.at[out_row(at)], out_keep.at[at]
        )

    def pass_on(source, at):
        pltpu.make_async_copy(source.at[at, side], rows_ref.at[out_row(at)], out_keep.at[at]).start()
        for peer in side_peers:
            pltpu.make_async_remote_copy(
                src_ref=source.at[at, peer],
                dst_ref=rows_ref.at[out_row(at)],
                send_sem=out_send.at[at],
                recv_sem=out_recv.at[at],
                device_id=on_side(peer),
                device_id_type=MESH,
            ).start()

    def relay(step, carry=0):
        at = plane(step)
        pltpu.make_async_copy(passing.at[at], passing.at[at], row_recv.at[at]).wait()
        pass_on(passing, at)
        return carry

    pass_on(packed, z)

    def tally_copy(peer):
        return pltpu.make_async_remote_copy(
            src_ref=tally_all.at[y],
            dst_ref=tally_all.at[y],
            send_sem=tally_send.at[peer],
            recv_sem=tally_recv.at[y],
            device_id=on_rep(peer),
            device_id_type=MESH,
        )

    def part_copy(source, parts, me, peer, place, send, recv):
        return pltpu.make_async_remote_copy(
            src_ref=source.at[0],
            dst_ref=parts.at[me],
            send_sem=send.at[peer],
            recv_sem=recv.at[me],
            device_id=place(peer),
            device_id_type=MESH,
        )

    def part_arrive(parts, peer, recv):
        pltpu.make_async_copy(parts.at[peer], parts.at[peer], recv.at[peer]).wait()

    def lanes_of(count):
        return lax.broadcasted_iota(jnp.int32, (count, 1, LANES), 2)

    for peer in rep_peers:
        part_copy(own_row, parts_rep, y, peer, on_rep, rep_send, rep_recv).start()
    for peer in rep_peers:
        tally_copy(peer).start()
    for peer in rep_peers:
        part_arrive(parts_rep, peer, rep_recv)
    side_row[...] = merged(parts_rep[...], lanes_of(count_y))
    parts_side[side] = side_row[0]
    for peer in rep_peers:
        pltpu.make_async_copy(tally_all.at[peer], tally_all.at[peer], tally_recv.at[peer]).wait()
    counts_ref[...] = jnp.sum(tally_all[...], axis=0)
    for peer in side_peers:
        part_copy(side_row, parts_side, side, peer, on_side, side_send, side_recv).start()
    for peer in side_peers:
        part_arrive(parts_side, peer, side_recv)
    plane_row[...] = merged(parts_side[...], lanes_of(count_s))
    parts_ring[z] = plane_row[0]
    if held_back < count_z - 1:
        relay(held_back)
    for peer in ring_peers:
        part_copy(plane_row, parts_ring, z, peer, on_ring, ring_send, ring_recv).start()
    for step in range(1, held_back):
        row_copy(plane(step)).start()
    first_rest = held_back + 1 if held_back < count_z - 1 else held_back
    lax.fori_loop(first_rest, count_z, relay, 0)
    for step in range(1, held_back):
        relay(step)
    for peer in ring_peers:
        part_arrive(parts_ring, peer, ring_recv)
    whole = merged(parts_ring[...], lanes_of(count_z))
    moments_ref[...] = whole[0]

    def finish(at, carry):
        several_ids = asked.at[at, pl.ds(0, count_s - 1)]
        pltpu.make_async_copy(several_ids, several_ids, ask_send.at[at]).wait()
        several_rows = rows_ref.at[pl.ds(0, count_s - 1)]
        pltpu.make_async_copy(several_rows, several_rows, out_send.at[at]).wait()
        pltpu.make_async_copy(several_rows, several_rows, out_recv.at[at]).wait()
        out_keep_copy(at).wait()
        return carry

    lax.fori_loop(0, count_z, finish, 0)

    def sent(step, carry):
        at = plane(step)
        ids_copy(at).wait_send()
        row_copy(at).wait_send()
        return carry

    lax.fori_loop(1, count_z, sent, 0)
    for peer in ring_peers:
        part_copy(plane_row, parts_ring, z, peer, on_ring, ring_send, ring_recv).wait_send()
    for peer in side_peers:
        part_copy(side_row, parts_side, side, peer, on_side, side_send, side_recv).wait_send()
    for peer in rep_peers:
        part_copy(own_row, parts_rep, y, peer, on_rep, rep_send, rep_recv).wait_send()
        tally_copy(peer).wait_send()


def per_device(requests, request_counts, table, gain):
    sizes = tuple(lax.axis_size(axis) for axis in ROWS_REP)
    count_x, count_z, count_c, count_y = sizes
    count_s = count_x * count_c
    owners, slots = requests.shape[1:]
    held, width = table.shape
    slot = lax.broadcasted_iota(jnp.int32, (owners, slots), 1)
    live = slot < request_counts[0][:, None]
    ids = jnp.where(live, requests[0], -1).reshape(count_x, count_z, count_c, slots)
    ids = ids.transpose(1, 0, 2, 3).reshape(count_z, 1, count_s * slots)
    ids = jnp.pad(ids, ((0, 0), (0, 0), (0, LANES - count_s * slots)), constant_values=-1)

    dma = pltpu.SemaphoreType.DMA
    vmem = pltpu.VMEM
    rows, tally, moments = pl.pallas_call(
        functools.partial(exchange, sizes, slots),
        out_shape=(
            jax.ShapeDtypeStruct((owners, slots, width), jnp.bfloat16),
            jax.ShapeDtypeStruct((1, held), jnp.int32),
            jax.ShapeDtypeStruct((1, LANES), jnp.float32),
        ),
        in_specs=[
            pl.BlockSpec(memory_space=pltpu.VMEM),
            pl.BlockSpec(memory_space=pl.ANY),
        ],
        out_specs=(
            pl.BlockSpec(memory_space=pl.ANY),
            pl.BlockSpec(memory_space=pltpu.VMEM),
            pl.BlockSpec(memory_space=pltpu.VMEM),
        ),
        scratch_shapes=[
            vmem((held, width), jnp.bfloat16),
            vmem((count_z, 1, LANES), jnp.int32),
            vmem((count_z, count_s, 1, LANES), jnp.int32),
            vmem((count_z, count_s * slots, LANES), jnp.float32),
            vmem((count_z, count_s, slots, width), jnp.bfloat16),
            vmem((count_z, count_s, slots, width), jnp.bfloat16),
            vmem((slots, width), jnp.float32),
            vmem((8, held), jnp.float32),
            vmem((count_y, 1, held), jnp.int32),
            vmem((1, 1, LANES), jnp.float32),
            vmem((1, 1, LANES), jnp.float32),
            vmem((1, 1, LANES), jnp.float32),
            vmem((count_y, 1, LANES), jnp.float32),
            vmem((count_s, 1, LANES), jnp.float32),
            vmem((count_z, 1, LANES), jnp.float32),
            dma((2,)),
            dma((count_z,)),
            dma((count_z,)),
            dma((count_z,)),
            dma((count_z,)),
            dma((count_z,)),
            dma((count_z,)),
            dma((count_z,)),
            dma((count_z,)),
            dma((count_z,)),
            dma((count_z,)),
            dma((count_y,)),
            dma((count_y,)),
            dma((count_y,)),
            dma((count_y,)),
            dma((count_s,)),
            dma((count_s,)),
            dma((count_z,)),
            dma((count_z,)),
        ],
        compiler_params=pltpu.CompilerParams(collective_id=0, has_side_effects=True),
    )(ids, table)

    entries = moments[0, 0]
    layer_mean = moments[0, 1 : 1 + LAYERS]
    layer_var = moments[0, 1 + LAYERS : 1 + 2 * LAYERS] / entries
    inverse = jnp.repeat(lax.rsqrt(layer_var + epsilon), WIDTH) * gain
    finished = (rows.astype(jnp.float32) - jnp.repeat(layer_mean, WIDTH)) * inverse
    normalized = jnp.where(live[..., None], finished, 0.0).astype(jnp.bfloat16)
    return (normalized[None], tally[0], jnp.stack([layer_mean, layer_var]))


def solution(mesh):
    count_y = mesh.shape["rep"]
    cores = 2
    count_x = mesh.devices.shape[0] // (16 * cores)
    finer = Mesh(mesh.devices.reshape(count_x, 16, cores, count_y), ROWS_REP)
    placed = (P(ROWS_REP, None, None), P(ROWS_REP, None), P(ROWS, None), P())
    return jax.shard_map(
        per_device,
        mesh=finer,
        in_specs=placed,
        out_specs=(P(ROWS_REP, None, None, None), P(ROWS), P()),
        check_vma=False,
    )
```

time: 135 us -> 90.2 us (0.67)
  blocking collectives: 101 us -> 0 us
  Pallas kernels: 0 us -> 79.3 us
  starting transfers between devices: 12.1 us -> 0 us
  local copies, waits for them, and re-layouts: 9.04 us -> 2.88 us
  other arithmetic: 10.5 us -> 6.61 us
    pallas_call x0 -> x1, Pallas kernels: none -> 79.3 us  [per_device(): pl.pallas_call(functools.partial(exchange, sizes, slots), out_shape=(jax....]
    all_gather x3 -> x0, blocking collectives: 65.3 us -> none  [collected_together(): both, at, found = (lax.all_gather(jnp.concatenate(lines), axis), 0, {})]
    all_to_all x1 -> x0, blocking collectives: 35.2 us -> none  [sent_together(): lax.all_to_all(both, axis, split_axis=split_dim, concat_axis=concat_dim,...]
    all_to_all x2 -> x0, starting transfers between devices: 12.1 us -> none  [the longest x1 7.93 us: per_device(): lax.all_to_all(looked, ROWS, split_axis=0, concat_axis=1, tiled=True)]
    gather x1 -> x0, local copies, waits for them, and re-layouts: 5.35 us -> none  [per_device(): jnp.take(table, row_index, axis=0)]
    reduce_sum x5 -> x0, other arithmetic: 3.82 us -> none  [the longest x1 1.26 us: per_device(): jnp.sum(jnp.square(shaped.astype(jnp.float32) - mean_here[None, :, None])...]
    convert_element_type x2 -> x0, other arithmetic: 2.56 us -> none  [the longest x1 2.55 us: per_device(): jnp.where(own_live[..., None], finished, 0.0).astype(jnp.bfloat16)]
    broadcast_in_dim x0 -> x1, other arithmetic: none -> 2.56 us  [per_device(): return (normalized[None], tally[0], jnp.stack([layer_mean, layer_var]))]
  transfers between devices with their start and end apart: 2 -> 0, of which waited for: 0 -> 0; matrix products, arithmetic and copies ran while one was open for 11% -> 0% of each run, Pallas kernels for 0% -> 0%
where the time goes in v1:
time: 90.2 us; the launch traced here: 89.5 us
  Pallas kernels  79.3 us (88%)
  other arithmetic  6.61 us (7%)
  local copies, waits for them, and re-layouts  2.88 us (3%)
    pallas_call x1, Pallas kernels, per_device(): pl.pallas_call(functools.partial(exchange, sizes, slots), out_shape=(jax....  79.3 us
    broadcast_in_dim x1, other arithmetic, per_device(): return (normalized[None], tally[0], jnp.stack([layer_mean, layer_var]))  2.56 us
    unnamed x10, local copies, waits for them, and re-layouts  1.98 us

profile of v1, /device:TPU:1, one launch (start us, length us, event | category | flops | bytes accessed | tf_op | source)
XLA Modules:
  0.0 89.5 jit_solution(18346542235774587895)
XLA Ops:
  0.6 0.0 copy-start.1
  0.6 0.5 broadcast.30
  1.2 1.3 %reduce.3 = s32[128]{0:T(128)S(1)} reduce(s32[1,128]{1,0:T(1,128)} %param.5, s32[]{:T(128)} %broadcast.30), dimensions={0}, to_apply=%param.5.reduce_sub_computation.3 | reduce | bytes 1028 | tf_op args[1]
  2.5 0.7 iota_compare_fusion
  3.2 0.1 lt.24
  3.3 0.8 copy.9
  4.1 0.1 fusion.1
  4.3 0.1 copy.10
  4.4 0.1 copy.11
  4.4 0.6 pad.4.ids_ref
  5.1 79.3 %shard_map.67 = (bf16[128,8,512]{2,1,0:T(8,128)(2,1)}, s32[1,1024]{1,0:T(1,128)}, f32[1,128]{1,0:T(1,128)}) custom-call(s32[16,1,128]{2,1,0:T(1,128)} %pad.4.ids_ref, bf16[1024,512]{1,0:T(8,128)(2,1)} %table_ref.1), custom_call_target="tpu_custom_call" | custom-call | tf_op jit(solution)/shard_map/pallas_call | solution.py:393
  84.3 1.3 %fusion.2 = (f32[1,2]{1,0:T(1,128)S(1)}, f32[2]{0:T(128)S(1)}, f32[2]{0:T(128)S(1)}, f32[1,2]{1,0:T(1,128)S(1)}) fusion(f32[1,128]{1,0:T(1,128)} %get-tuple-element.7, f32[]{:T(128)} %bitcast.24), kind=kLoop, calls=%fused_computation.11 | loop fusion | flops 4 | bytes 52 | tf_op jit(solution)/shard_map/slice | solution.py:449
  85.6 0.6 pad_maximum_fusion
  86.2 0.1 broadcast_bitcast_fusion
  86.3 0.0 copy-done.1
  86.3 0.0 copy-start
  86.3 2.6 %fusion = bf16[1,128,8,512]{3,2,1,0:T(8,128)(2,1)} fusion(bf16[128,8,512]{2,1,0:T(8,128)(2,1)} %get-tuple-element.6, f32[512]{0:T(512)S(1)} %mul.11, f32[512]{0:T(512)S(1)} %bitcast.23, pred[128,8]{1,0:T(8,128)(4,1)S(1)} %iota_compare_fusion), kind=kLoop, calls=%fused_computation.1 | loop fusion | flops 2621440 | bytes 2102272 | tf_op jit(solution)/shard_map/broadcast_in_dim | solution.py:454
  88.9 0.0 copy-done
  88.9 0.6 copy.15
  (3 shorter events, 0.0 us)
Async XLA Ops:
  0.6 85.7 %copy-start.1 = (f32[512]{0:T(512)S(1)}, f32[512]{0:T(512)}, u32[]{:S(2)}) copy-start(f32[512]{0:T(512)} %param.7) | copy-start | bytes 6148
  86.3 2.6 %copy-start = (s32[1,1024]{1,0:T(1,128)S(1)}, s32[1,1024]{1,0:T(1,128)}, u32[]{:S(2)}) copy-start(s32[1,1024]{1,0:T(1,128)} %get-tuple-element.8) | copy-start | bytes 12292

commit v2 on v1

--- a/solution.py
+++ b/solution.py
@@ -43,17 +43,23 @@
 def exchange(
     sizes,
     slots,
-    ids_ref,
+    requests_ref,
+    used_ref,
+    gain_ref,
     table_ref,
     rows_ref,
     counts_ref,
     moments_ref,
+    affine_ref,
     table,
+    upright,
+    ids_ref,
     heard,
     asked,
     column,
     packed,
     passing,
+    turned,
     totals,
     tally,
     tally_all,
@@ -71,6 +77,9 @@
     ask_recv,
     row_send,
     row_recv,
+    turn_send,
+    turn_recv,
+    turn_keep,
     out_send,
     out_recv,
     out_keep,
@@ -113,8 +122,6 @@
 
     load_table = pltpu.make_async_copy(table_ref, table, local_sem.at[0])
     load_table.start()
-    load_ids = pltpu.make_async_copy(ids_ref.at[z], heard.at[z], local_sem.at[1])
-    load_ids.start()
 
     barrier = pltpu.get_barrier_semaphore()
     for peer in ring_peers:
@@ -123,6 +130,19 @@
         pl.semaphore_signal(barrier, inc=1, device_id=on_side(peer), device_id_type=MESH)
     for peer in rep_peers:
         pl.semaphore_signal(barrier, inc=1, device_id=on_rep(peer), device_id_type=MESH)
+
+    slot = lax.broadcasted_iota(jnp.int32, requests_ref.shape, 0)
+    ids = jnp.where(slot < used_ref[...], requests_ref[...], -1)
+    owners = ids.shape[1]
+    ids = jnp.concatenate([ids, jnp.zeros((LANES - slots, owners), jnp.int32)], axis=0)
+    upright[...] = jnp.transpose(ids)
+    lines = jnp.zeros((count_z, LANES), jnp.int32)
+    for at in range(count_s):
+        first = (at // count_c) * count_z * count_c + at % count_c
+        line = upright[pl.ds(first, count_z, stride=count_c), :]
+        lines += pltpu.roll(line, slots * at, 1) if at else line
+    ids_ref[...] = lines.reshape(count_z, 1, LANES)
+
     pl.semaphore_wait(barrier, len(ring_peers) + len(side_peers) + len(rep_peers))
 
     def ids_copy(at):
@@ -191,7 +211,7 @@
         )
         found = jnp.dot(hot, table[...], preferred_element_type=jnp.float32)
         found = found.reshape(count_s, slots, width)
-        packed[at] = found.astype(jnp.bfloat16)
+        packed[at] = found.astype(jnp.bfloat16).reshape(count_x, count_c, slots, width)
         totals[...] += jnp.sum(found, axis=0)
         ones = jnp.ones((8, count_s * slots), jnp.bfloat16)
         tally[...] += jnp.dot(ones, hot, preferred_element_type=jnp.float32)
@@ -207,15 +227,78 @@
             device_id_type=MESH,
         )
 
-    held_back = min(3, count_z - 1)
-
-    def give(step):
-        @pl.when(step >= held_back)
+    def turn_keep_copy(at):
+        return pltpu.make_async_copy(packed.at[at, x, c], turned.at[at, x, c], turn_keep.at[at])
+
+    def turn(at):
+        turn_keep_copy(at).start()
+        for peer in side_peers:
+            px, pc = lax.div(peer, count_c), lax.rem(peer, count_c)
+            pltpu.make_async_remote_copy(
+                src_ref=packed.at[at, px, pc],
+                dst_ref=turned.at[at, x, c],
+                send_sem=turn_send.at[at],
+                recv_sem=turn_recv.at[at],
+                device_id=on_side(peer),
+                device_id_type=MESH,
+            ).start()
+
+    def pass_on(source, at):
+        pltpu.make_async_copy(source.at[at, x, c], rows_ref.at[x, at, c], out_keep.at[at]).start()
+        for peer in side_peers:
+            px, pc = lax.div(peer, count_c), lax.rem(peer, count_c)
+            pltpu.make_async_remote_copy(
+                src_ref=source.at[at, px, pc],
+                dst_ref=rows_ref.at[x, at, c],
+                send_sem=out_send.at[at],
+                recv_sem=out_recv.at[at],
+                device_id=on_side(peer),
+                device_id_type=MESH,
+            ).start()
+
+    def last_copy(at):
+        return pltpu.make_async_remote_copy(
+            src_ref=turned.at[at],
+            dst_ref=rows_ref.at[:, z],
+            send_sem=row_send.at[at],
+            recv_sem=row_recv.at[z],
+            device_id=on_ring(at),
+            device_id_type=MESH,
+        )
+
+    def side_bytes(sem, at):
+        several = passing.at[pl.ds(0, count_s - 1), 0, 0]
+        pltpu.make_async_copy(several, several, sem.at[at]).wait()
+
+    def last(step, carry=0):
+        at = plane(step)
+        turn_keep_copy(at).wait()
+        side_bytes(turn_recv, at)
+        last_copy(at).start()
+        return carry
+
+    relayed = min(6, (count_z - 3) // 2 * 2)
+    early = min(3, count_z - 1 - relayed)
+
+    def give(step, carry=0):
+        at = plane(step)
+
+        @pl.when(step == 0)
         def _():
-            row_copy(plane(step)).start()
+            pass_on(packed, at)
+
+        @pl.when((step >= 1) & (step <= relayed))
+        def _():
+            row_copy(at).start()
+
+        @pl.when(step > relayed)
+        def _():
+            turn(at)
+
+        return carry
 
     ahead = min(5, count_z - 2)
-    load_ids.wait()
+    heard[z] = ids_ref[z]
     tell(z)
     lax.fori_loop(1, ahead + 1, hear, 0)
     load_table.wait()
@@ -231,7 +314,9 @@
         give(step - 1)
         return carry
 
-    lax.fori_loop(0, count_z - 1 - ahead, both, 0)
+    look(0)
+    hear(ahead + 1)
+    lax.fori_loop(1, count_z - 1 - ahead, both, 0)
     lax.fori_loop(count_z - 1 - ahead, count_z, only, 0)
 
     tally_all[y] = tally[0:1].astype(jnp.int32)
@@ -249,7 +334,8 @@
         used = column[at] >= 0.0
         used = jnp.concatenate([used.astype(jnp.float32)] * (width // LANES), axis=1)
         used = used.reshape(count_s, slots, width)
-        away = (packed[at].astype(jnp.float32) - center[None]) * used
+        rows = packed[at].reshape(count_s, slots, width).astype(jnp.float32)
+        away = (rows - center[None]) * used
         return total + jnp.sum(away * away, axis=0)
 
     spread = lax.fori_loop(0, count_z, squares, jnp.zeros((slots, width), jnp.float32))
@@ -263,33 +349,14 @@
     own_row[...] = row[None]
     parts_rep[y] = row
 
-    def out_row(at):
-        return (x * count_z + at) * count_c + c
-
-    def out_keep_copy(at):
-        return pltpu.make_async_copy(
-            passing.at[at, side], rows_ref.at[out_row(at)], out_keep.at[at]
-        )
-
-    def pass_on(source, at):
-        pltpu.make_async_copy(source.at[at, side], rows_ref.at[out_row(at)], out_keep.at[at]).start()
-        for peer in side_peers:
-            pltpu.make_async_remote_copy(
-                src_ref=source.at[at, peer],
-                dst_ref=rows_ref.at[out_row(at)],
-                send_sem=out_send.at[at],
-                recv_sem=out_recv.at[at],
-                device_id=on_side(peer),
-                device_id_type=MESH,
-            ).start()
-
     def relay(step, carry=0):
         at = plane(step)
         pltpu.make_async_copy(passing.at[at], passing.at[at], row_recv.at[at]).wait()
         pass_on(passing, at)
         return carry
 
-    pass_on(packed, z)
+    for step in range(count_z - 1, count_z - 1 - early, -1):
+        last(step)
 
     def tally_copy(peer):
         return pltpu.make_async_remote_copy(
@@ -334,28 +401,49 @@
         part_arrive(parts_side, peer, side_recv)
     plane_row[...] = merged(parts_side[...], lanes_of(count_s))
     parts_ring[z] = plane_row[0]
-    if held_back < count_z - 1:
-        relay(held_back)
+    relay(1)
     for peer in ring_peers:
         part_copy(plane_row, parts_ring, z, peer, on_ring, ring_send, ring_recv).start()
-    for step in range(1, held_back):
-        row_copy(plane(step)).start()
-    first_rest = held_back + 1 if held_back < count_z - 1 else held_back
-    lax.fori_loop(first_rest, count_z, relay, 0)
-    for step in range(1, held_back):
-        relay(step)
+    for step in range(count_z - 1 - early, relayed, -1):
+        last(step)
+    lax.fori_loop(2, relayed + 1, relay, 0)
     for peer in ring_peers:
         part_arrive(parts_ring, peer, ring_recv)
-    whole = merged(parts_ring[...], lanes_of(count_z))
-    moments_ref[...] = whole[0]
-
-    def finish(at, carry):
+    whole = merged(parts_ring[...], lanes_of(count_z))[0]
+
+    def lone(at):
+        return jnp.sum(jnp.where(lane == at, whole, 0.0), axis=1, keepdims=True)
+
+    entries = lone(0)
+    mean = [lone(1 + layer) for layer in range(LAYERS)]
+    var = [lone(1 + LAYERS + layer) / entries for layer in range(LAYERS)]
+    pair = lax.broadcasted_iota(jnp.int32, (1, LAYERS), 1)
+    for row, values in enumerate((mean, var)):
+        line = jnp.zeros((1, LAYERS), jnp.float32)
+        for layer in range(LAYERS):
+            line = jnp.where(pair == layer, values[layer], line)
+        moments_ref[row : row + 1] = line
+    for layer in range(LAYERS):
+        span = slice(layer * WIDTH, (layer + 1) * WIDTH)
+        affine_ref[0:1, span] = jnp.broadcast_to(mean[layer], (1, WIDTH))
+        affine_ref[1:2, span] = lax.rsqrt(var[layer] + epsilon) * gain_ref[:, span]
+
+    def finish(step, carry):
+        at = plane(step)
         several_ids = asked.at[at, pl.ds(0, count_s - 1)]
         pltpu.make_async_copy(several_ids, several_ids, ask_send.at[at]).wait()
-        several_rows = rows_ref.at[pl.ds(0, count_s - 1)]
-        pltpu.make_async_copy(several_rows, several_rows, out_send.at[at]).wait()
-        pltpu.make_async_copy(several_rows, several_rows, out_recv.at[at]).wait()
-        out_keep_copy(at).wait()
+
+        @pl.when(step <= relayed)
+        def _():
+            side_bytes(out_send, at)
+            side_bytes(out_recv, at)
+            pltpu.make_async_copy(packed.at[at, x, c], rows_ref.at[x, at, c], out_keep.at[at]).wait()
+
+        @pl.when(step > relayed)
+        def _():
+            side_bytes(turn_send, at)
+            pltpu.make_async_copy(passing.at[at], passing.at[at], row_recv.at[at]).wait()
+
         return carry
 
     lax.fori_loop(0, count_z, finish, 0)
@@ -363,7 +451,7 @@
     def sent(step, carry):
         at = plane(step)
         ids_copy(at).wait_send()
-        row_copy(at).wait_send()
+        pltpu.make_async_copy(passing.at[at], passing.at[at], row_send.at[at]).wait()
         return carry
 
     lax.fori_loop(1, count_z, sent, 0)
@@ -376,28 +464,40 @@
         tally_copy(peer).wait_send()
 
 
+def finished(used_ref, rows_ref, affine_ref, tally_ref, moments_ref, out_ref, counts_ref, result_ref):
+    block, slots, width = rows_ref.shape
+    slot = lax.broadcasted_iota(jnp.int32, (slots, width), 0)
+    mean = jnp.broadcast_to(affine_ref[0:1], (slots, width))
+    scale = jnp.broadcast_to(affine_ref[1:2], (slots, width))
+    first = pl.program_id(0) * block
+    for at in range(block):
+        value = (rows_ref[at].astype(jnp.float32) - mean) * scale
+        value = jnp.where(slot < used_ref[0, first + at], value, 0.0)
+        out_ref[at] = value.astype(jnp.bfloat16)
+    counts_ref[...] = tally_ref[...]
+    result_ref[...] = moments_ref[...]
+
+
 def per_device(requests, request_counts, table, gain):
     sizes = tuple(lax.axis_size(axis) for axis in ROWS_REP)
     count_x, count_z, count_c, count_y = sizes
     count_s = count_x * count_c
     owners, slots = requests.shape[1:]
     held, width = table.shape
-    slot = lax.broadcasted_iota(jnp.int32, (owners, slots), 1)
-    live = slot < request_counts[0][:, None]
-    ids = jnp.where(live, requests[0], -1).reshape(count_x, count_z, count_c, slots)
-    ids = ids.transpose(1, 0, 2, 3).reshape(count_z, 1, count_s * slots)
-    ids = jnp.pad(ids, ((0, 0), (0, 0), (0, LANES - count_s * slots)), constant_values=-1)
 
     dma = pltpu.SemaphoreType.DMA
     vmem = pltpu.VMEM
-    rows, tally, moments = pl.pallas_call(
+    rows, tally, moments, affine = pl.pallas_call(
         functools.partial(exchange, sizes, slots),
         out_shape=(
-            jax.ShapeDtypeStruct((owners, slots, width), jnp.bfloat16),
+            jax.ShapeDtypeStruct((count_x, count_z, count_c, slots, width), jnp.bfloat16),
             jax.ShapeDtypeStruct((1, held), jnp.int32),
-            jax.ShapeDtypeStruct((1, LANES), jnp.float32),
+            jax.ShapeDtypeStruct((2, LAYERS), jnp.float32),
+            jax.ShapeDtypeStruct((2, width), jnp.float32),
         ),
         in_specs=[
+            pl.BlockSpec(memory_space=pltpu.VMEM),
+            pl.BlockSpec(memory_space=pltpu.VMEM),
             pl.BlockSpec(memory_space=pltpu.VMEM),
             pl.BlockSpec(memory_space=pl.ANY),
         ],
@@ -405,14 +505,18 @@
             pl.BlockSpec(memory_space=pl.ANY),
             pl.BlockSpec(memory_space=pltpu.VMEM),
             pl.BlockSpec(memory_space=pltpu.VMEM),
+            pl.BlockSpec(memory_space=pltpu.VMEM),
         ),
         scratch_shapes=[
             vmem((held, width), jnp.bfloat16),
+            vmem((owners, LANES), jnp.int32),
+            vmem((count_z, 1, LANES), jnp.int32),
             vmem((count_z, 1, LANES), jnp.int32),
             vmem((count_z, count_s, 1, LANES), jnp.int32),
             vmem((count_z, count_s * slots, LANES), jnp.float32),
-            vmem((count_z, count_s, slots, width), jnp.bfloat16),
-            vmem((count_z, count_s, slots, width), jnp.bfloat16),
+            vmem((count_z, count_x, count_c, slots, width), jnp.bfloat16),
+            vmem((count_z, count_x, count_c, slots, width), jnp.bfloat16),
+            vmem((count_z, count_x, count_c, slots, width), jnp.bfloat16),
             vmem((slots, width), jnp.float32),
             vmem((8, held), jnp.float32),
             vmem((count_y, 1, held), jnp.int32),
@@ -422,7 +526,10 @@
             vmem((count_y, 1, LANES), jnp.float32),
             vmem((count_s, 1, LANES), jnp.float32),
             vmem((count_z, 1, LANES), jnp.float32),
-            dma((2,)),
+            dma((1,)),
+            dma((count_z,)),
+            dma((count_z,)),
+            dma((count_z,)),
             dma((count_z,)),
             dma((count_z,)),
             dma((count_z,)),
@@ -443,15 +550,32 @@
             dma((count_z,)),
         ],
         compiler_params=pltpu.CompilerParams(collective_id=0, has_side_effects=True),
-    )(ids, table)
-
-    entries = moments[0, 0]
-    layer_mean = moments[0, 1 : 1 + LAYERS]
-    layer_var = moments[0, 1 + LAYERS : 1 + 2 * LAYERS] / entries
-    inverse = jnp.repeat(lax.rsqrt(layer_var + epsilon), WIDTH) * gain
-    finished = (rows.astype(jnp.float32) - jnp.repeat(layer_mean, WIDTH)) * inverse
-    normalized = jnp.where(live[..., None], finished, 0.0).astype(jnp.bfloat16)
-    return (normalized[None], tally[0], jnp.stack([layer_mean, layer_var]))
+    )(requests[0].T, request_counts, gain[None], table)
+
+    steps = 4
+    block = owners // steps
+    rows, tally, moments = pl.pallas_call(
+        finished,
+        grid=(steps,),
+        out_shape=(
+            jax.ShapeDtypeStruct((owners, slots, width), jnp.bfloat16),
+            jax.ShapeDtypeStruct((1, held), jnp.int32),
+            jax.ShapeDtypeStruct((2, LAYERS), jnp.float32),
+        ),
+        in_specs=[
+            pl.BlockSpec(memory_space=pltpu.SMEM),
+            pl.BlockSpec((block, slots, width), lambda i: (i, 0, 0)),
+            pl.BlockSpec((2, width), lambda i: (0, 0)),
+            pl.BlockSpec((1, held), lambda i: (0, 0)),
+            pl.BlockSpec((2, LAYERS), lambda i: (0, 0)),
+        ],
+        out_specs=(
+            pl.BlockSpec((block, slots, width), lambda i: (i, 0, 0)),
+            pl.BlockSpec((1, held), lambda i: (0, 0)),
+            pl.BlockSpec((2, LAYERS), lambda i: (0, 0)),
+        ),
+    )(request_counts, rows.reshape(owners, slots, width), affine, tally, moments)
+    return (rows[None], tally[0], moments)
 
 
 def solution(mesh):

time: 90.2 us -> 84.6 us (0.938)
  other arithmetic: 6.61 us -> 0 us
  Pallas kernels: 79.3 us -> 83.8 us
  local copies, waits for them, and re-layouts: 2.88 us -> 0 us
    pallas_call x0 -> x1, Pallas kernels: none -> 3.54 us  [per_device(): pl.pallas_call(finished, grid=(steps,), out_shape=(jax.ShapeDtypeStruct((...]
    broadcast_in_dim x1 -> x0, other arithmetic: 2.56 us -> none  [per_device(): return (normalized[None], tally[0], jnp.stack([layer_mean, layer_var]))]
    unnamed x10 -> x0, local copies, waits for them, and re-layouts: 1.98 us -> none
    unnamed x1 -> x0, other arithmetic: 1.32 us -> none
    slice x1 -> x0, other arithmetic: 1.29 us -> none  [per_device(): layer_mean = moments[0, 1:1 + LAYERS]]
    pallas_call x1, Pallas kernels: 79.3 us -> 80.2 us  [per_device(): pl.pallas_call(functools.partial(exchange, sizes, slots), out_shape=(jax....]
where the time goes in v2:
time: 84.6 us; the launch traced here: 84.4 us
  Pallas kernels  83.8 us (99%)
    pallas_call x1, Pallas kernels, per_device(): pl.pallas_call(functools.partial(exchange, sizes, slots), out_shape=(jax....  80.2 us
    pallas_call x1, Pallas kernels, per_device(): pl.pallas_call(finished, grid=(steps,), out_shape=(jax.ShapeDtypeStruct((...  3.54 us

profile of v2, /device:TPU:1, one launch (start us, length us, event | category | flops | bytes accessed | tf_op | source)
XLA Modules:
  0.0 84.4 jit_solution(1130709146504817319)
XLA Ops:
  0.6 80.2 %shard_map.67 = (bf16[4,16,2,8,512]{4,3,2,1,0:T(8,128)(2,1)}, s32[1,1024]{1,0:T(1,128)}, f32[2,2]{1,0:T(2,128)}, f32[2,512]{1,0:T(2,128)}) custom-call(s32[8,128]{1,0:T(8,128)} %bitcast.8, s32[1,128]{1,0:T(1,128)} %used_ref.3, f32[1,512]{1,0:T(1,128)} %bitcast.9, bf16[1024,512]{1,0:T(8,128)(2,1)} %table_ref.1), custom_call_target="tpu_custom_call" | custom-call | tf_op jit(solution)/shard_map/pallas_call | solution.py:490
  80.9 3.5 %shard_map.68 = (bf16[128,8,512]{2,1,0:T(8,128)(2,1)}, s32[1,1024]{1,0:T(1,128)}, f32[2,2]{1,0:T(2,128)}) custom-call(s32[1,128]{1,0:T(1,128)} %used_ref.3, bf16[128,8,512]{2,1,0:T(8,128)(2,1)} %bitcast.7, f32[2,512]{1,0:T(2,128)} %get-tuple-element.11.affine_ref, s32[1,1024]{1,0:T(1,128)} %get-tuple-element.12.tally_ref, f32[2,2]{1,0:T(2,128)} %get-tuple-element.13.moments_ref), custom_call_target="tpu_custom_call" | custom-call | tf_op jit(solution)/shard_map/pallas_call | solution.py:557

commit v3 on v2

--- a/solution.py
+++ b/solution.py
@@ -14,6 +14,9 @@
 ROWS = ("rows_0", "rows_1", "rows_2")
 ROWS_REP = ("rows_0", "rows_1", "rows_2", "rep")
 MESH = pl.DeviceIdType.MESH
+LATE = (3, 1)
+BLOCKS = 4
+KERNEL_BYTES = 20 * 2**20
 
 epsilon = 1e-06
 
@@ -43,15 +46,19 @@
 def exchange(
     sizes,
     slots,
-    requests_ref,
-    used_ref,
-    gain_ref,
+    requests_hbm,
+    used_hbm,
+    gain_hbm,
     table_ref,
     rows_ref,
     counts_ref,
     moments_ref,
     affine_ref,
+    spread_ref,
     table,
+    requests_ref,
+    used_ref,
+    gain_ref,
     upright,
     ids_ref,
     heard,
@@ -120,8 +127,20 @@
         toward = 2 * lax.rem(step, 2) - 1
         return lax.rem(z + far * toward + count_z, count_z)
 
-    load_table = pltpu.make_async_copy(table_ref, table, local_sem.at[0])
-    load_table.start()
+    loads = [
+        pltpu.make_async_copy(source, target, local_sem.at[at])
+        for at, (source, target) in enumerate(
+            (
+                (requests_hbm, requests_ref),
+                (used_hbm, used_ref),
+                (gain_hbm, gain_ref),
+                (table_ref, table),
+            )
+        )
+    ]
+    for load in loads:
+        load.start()
+    load_table = loads.pop()
 
     barrier = pltpu.get_barrier_semaphore()
     for peer in ring_peers:
@@ -131,11 +150,14 @@
     for peer in rep_peers:
         pl.semaphore_signal(barrier, inc=1, device_id=on_rep(peer), device_id_type=MESH)
 
+    for load in loads:
+        load.wait()
     slot = lax.broadcasted_iota(jnp.int32, requests_ref.shape, 0)
     ids = jnp.where(slot < used_ref[...], requests_ref[...], -1)
     owners = ids.shape[1]
     ids = jnp.concatenate([ids, jnp.zeros((LANES - slots, owners), jnp.int32)], axis=0)
     upright[...] = jnp.transpose(ids)
+    spread_ref[...] = jnp.transpose(jnp.broadcast_to(used_ref[...], (LANES, owners)))
     lines = jnp.zeros((count_z, LANES), jnp.int32)
     for at in range(count_s):
         first = (at // count_c) * count_z * count_c + at % count_c
@@ -277,8 +299,15 @@
         last_copy(at).start()
         return carry
 
-    relayed = min(6, (count_z - 3) // 2 * 2)
-    early = min(3, count_z - 1 - relayed)
+    def is_late(step):
+        far = lax.div(step + 1, 2)
+        found = far == LATE[0]
+        for distance in LATE[1:]:
+            found = found | (far == distance)
+        return found
+
+    late_steps = [2 * far - side for far in LATE for side in (1, 0)]
+    soon_steps = [step for step in range(1, count_z) if step not in late_steps]
 
     def give(step, carry=0):
         at = plane(step)
@@ -287,11 +316,11 @@
         def _():
             pass_on(packed, at)
 
-        @pl.when((step >= 1) & (step <= relayed))
+        @pl.when((step >= 1) & jnp.logical_not(is_late(step)))
         def _():
             row_copy(at).start()
 
-        @pl.when(step > relayed)
+        @pl.when(is_late(step))
         def _():
             turn(at)
 
@@ -351,12 +380,16 @@
 
     def relay(step, carry=0):
         at = plane(step)
+
+        @pl.when(jnp.logical_not(is_late(step)))
+        def _():
+            relay_plane(at)
+
+        return carry
+
+    def relay_plane(at):
         pltpu.make_async_copy(passing.at[at], passing.at[at], row_recv.at[at]).wait()
         pass_on(passing, at)
-        return carry
-
-    for step in range(count_z - 1, count_z - 1 - early, -1):
-        last(step)
 
     def tally_copy(peer):
         return pltpu.make_async_remote_copy(
@@ -401,12 +434,12 @@
         part_arrive(parts_side, peer, side_recv)
     plane_row[...] = merged(parts_side[...], lanes_of(count_s))
     parts_ring[z] = plane_row[0]
-    relay(1)
+    relay_plane(plane(soon_steps[0]))
     for peer in ring_peers:
         part_copy(plane_row, parts_ring, z, peer, on_ring, ring_send, ring_recv).start()
-    for step in range(count_z - 1 - early, relayed, -1):
+    for step in late_steps:
         last(step)
-    lax.fori_loop(2, relayed + 1, relay, 0)
+    lax.fori_loop(soon_steps[0] + 1, count_z, relay, 0)
     for peer in ring_peers:
         part_arrive(parts_ring, peer, ring_recv)
     whole = merged(parts_ring[...], lanes_of(count_z))[0]
@@ -433,13 +466,13 @@
         several_ids = asked.at[at, pl.ds(0, count_s - 1)]
         pltpu.make_async_copy(several_ids, several_ids, ask_send.at[at]).wait()
 
-        @pl.when(step <= relayed)
+        @pl.when(jnp.logical_not(is_late(step)))
         def _():
             side_bytes(out_send, at)
             side_bytes(out_recv, at)
             pltpu.make_async_copy(packed.at[at, x, c], rows_ref.at[x, at, c], out_keep.at[at]).wait()
 
-        @pl.when(step > relayed)
+        @pl.when(is_late(step))
         def _():
             side_bytes(turn_send, at)
             pltpu.make_async_copy(passing.at[at], passing.at[at], row_recv.at[at]).wait()
@@ -464,18 +497,30 @@
         tally_copy(peer).wait_send()
 
 
-def finished(used_ref, rows_ref, affine_ref, tally_ref, moments_ref, out_ref, counts_ref, result_ref):
-    block, slots, width = rows_ref.shape
+def finished(spread_ref, rows_ref, affine_ref, tally_ref, moments_ref, out_hbm, counts_ref, result_ref, done, done_sem):
+    owners, slots, width = rows_ref.shape
+    block = owners // BLOCKS
     slot = lax.broadcasted_iota(jnp.int32, (slots, width), 0)
     mean = jnp.broadcast_to(affine_ref[0:1], (slots, width))
     scale = jnp.broadcast_to(affine_ref[1:2], (slots, width))
-    first = pl.program_id(0) * block
-    for at in range(block):
-        value = (rows_ref[at].astype(jnp.float32) - mean) * scale
-        value = jnp.where(slot < used_ref[0, first + at], value, 0.0)
-        out_ref[at] = value.astype(jnp.bfloat16)
+
+    def send(part):
+        span = pl.ds(part * block, block)
+        return pltpu.make_async_copy(done.at[span], out_hbm.at[span], done_sem.at[part])
+
+    for part in range(BLOCKS):
+        for at in range(part * block, (part + 1) * block):
+            value = (rows_ref[at].astype(jnp.float32) - mean) * scale
+            used = jnp.concatenate([spread_ref[at : at + 1]] * (width // LANES), axis=1)
+            value = jnp.where(slot < used, value, 0.0)
+            done[at] = value.astype(jnp.bfloat16)
+        if part:
+            send(part - 1).start()
     counts_ref[...] = tally_ref[...]
     result_ref[...] = moments_ref[...]
+    send(BLOCKS - 1).start()
+    for part in range(BLOCKS):
+        send(part).wait()
 
 
 def per_device(requests, request_counts, table, gain):
@@ -487,28 +532,28 @@
 
     dma = pltpu.SemaphoreType.DMA
     vmem = pltpu.VMEM
-    rows, tally, moments, affine = pl.pallas_call(
+    rows, tally, moments, affine, spread = pl.pallas_call(
         functools.partial(exchange, sizes, slots),
         out_shape=(
             jax.ShapeDtypeStruct((count_x, count_z, count_c, slots, width), jnp.bfloat16),
             jax.ShapeDtypeStruct((1, held), jnp.int32),
             jax.ShapeDtypeStruct((2, LAYERS), jnp.float32),
             jax.ShapeDtypeStruct((2, width), jnp.float32),
+            jax.ShapeDtypeStruct((owners, LANES), jnp.int32),
         ),
-        in_specs=[
-            pl.BlockSpec(memory_space=pltpu.VMEM),
-            pl.BlockSpec(memory_space=pltpu.VMEM),
-            pl.BlockSpec(memory_space=pltpu.VMEM),
-            pl.BlockSpec(memory_space=pl.ANY),
-        ],
+        in_specs=[pl.BlockSpec(memory_space=pltpu.HBM)] * 4,
         out_specs=(
             pl.BlockSpec(memory_space=pl.ANY),
+            pl.BlockSpec(memory_space=pltpu.VMEM),
             pl.BlockSpec(memory_space=pltpu.VMEM),
             pl.BlockSpec(memory_space=pltpu.VMEM),
             pl.BlockSpec(memory_space=pltpu.VMEM),
         ),
         scratch_shapes=[
             vmem((held, width), jnp.bfloat16),
+            vmem((slots, owners), jnp.int32),
+            vmem((1, owners), jnp.int32),
+            vmem((1, width), jnp.float32),
             vmem((owners, LANES), jnp.int32),
             vmem((count_z, 1, LANES), jnp.int32),
             vmem((count_z, 1, LANES), jnp.int32),
@@ -526,7 +571,7 @@
             vmem((count_y, 1, LANES), jnp.float32),
             vmem((count_s, 1, LANES), jnp.float32),
             vmem((count_z, 1, LANES), jnp.float32),
-            dma((1,)),
+            dma((4,)),
             dma((count_z,)),
             dma((count_z,)),
             dma((count_z,)),
@@ -549,32 +594,32 @@
             dma((count_z,)),
             dma((count_z,)),
         ],
-        compiler_params=pltpu.CompilerParams(collective_id=0, has_side_effects=True),
-    )(requests[0].T, request_counts, gain[None], table)
-
-    steps = 4
-    block = owners // steps
+        compiler_params=pltpu.CompilerParams(
+            collective_id=0, has_side_effects=True, vmem_limit_bytes=KERNEL_BYTES
+        ),
+    )(
+        *[
+            pltpu.with_memory_space_constraint(value, pltpu.HBM)
+            for value in (requests[0].T, request_counts, gain[None], table)
+        ]
+    )
+
     rows, tally, moments = pl.pallas_call(
         finished,
-        grid=(steps,),
         out_shape=(
             jax.ShapeDtypeStruct((owners, slots, width), jnp.bfloat16),
             jax.ShapeDtypeStruct((1, held), jnp.int32),
             jax.ShapeDtypeStruct((2, LAYERS), jnp.float32),
         ),
-        in_specs=[
-            pl.BlockSpec(memory_space=pltpu.SMEM),
-            pl.BlockSpec((block, slots, width), lambda i: (i, 0, 0)),
-            pl.BlockSpec((2, width), lambda i: (0, 0)),
-            pl.BlockSpec((1, held), lambda i: (0, 0)),
-            pl.BlockSpec((2, LAYERS), lambda i: (0, 0)),
-        ],
+        in_specs=[pl.BlockSpec(memory_space=pltpu.VMEM)] * 5,
         out_specs=(
-            pl.BlockSpec((block, slots, width), lambda i: (i, 0, 0)),
-            pl.BlockSpec((1, held), lambda i: (0, 0)),
-            pl.BlockSpec((2, LAYERS), lambda i: (0, 0)),
+            pl.BlockSpec(memory_space=pltpu.HBM),
+            pl.BlockSpec(memory_space=pltpu.VMEM),
+            pl.BlockSpec(memory_space=pltpu.VMEM),
         ),
-    )(request_counts, rows.reshape(owners, slots, width), affine, tally, moments)
+        scratch_shapes=[vmem((owners, slots, width), jnp.bfloat16), dma((BLOCKS,))],
+        compiler_params=pltpu.CompilerParams(vmem_limit_bytes=KERNEL_BYTES),
+    )(spread, rows.reshape(owners, slots, width), affine, tally, moments)
     return (rows[None], tally[0], moments)
 
 

time: 84.6 us -> 79 us (0.934)
  Pallas kernels: 83.8 us -> 77.5 us
    pallas_call x1, Pallas kernels: 80.2 us -> 75.8 us  [per_device(): pl.pallas_call(functools.partial(exchange, sizes, slots), out_shape=(jax....]
    pallas_call x1, Pallas kernels: 3.54 us -> 1.76 us  [per_device(): pl.pallas_call(finished, out_shape=(jax.ShapeDtypeStruct((owners, slots,...]
where the time goes in v3:
time: 79 us; the launch traced here: 78.2 us
  Pallas kernels  77.5 us (98%)
    pallas_call x1, Pallas kernels, per_device(): pl.pallas_call(functools.partial(exchange, sizes, slots), out_shape=(jax....  75.8 us
    pallas_call x1, Pallas kernels, per_device(): pl.pallas_call(finished, out_shape=(jax.ShapeDtypeStruct((owners, slots,...  1.76 us

profile of v3, /device:TPU:1, one launch (start us, length us, event | category | flops | bytes accessed | tf_op | source)
XLA Modules:
  0.0 78.2 jit_solution(1195326592934640356)
XLA Ops:
  0.6 75.8 %shard_map.67 = (bf16[4,16,2,8,512]{4,3,2,1,0:T(8,128)(2,1)S(1)}, s32[1,1024]{1,0:T(1,128)S(1)}, f32[2,2]{1,0:T(2,128)S(1)}, f32[2,512]{1,0:T(2,128)S(1)}, s32[128,128]{1,0:T(8,128)S(1)}) custom-call(s32[8,128]{1,0:T(8,128)} %bitcast.8, s32[1,128]{1,0:T(1,128)} %used_hbm.1, f32[1,512]{1,0:T(1,128)} %bitcast.9, bf16[1024,512]{1,0:T(8,128)(2,1)} %table_ref.1), custom_call_target="tpu_custom_call" | custom-call | tf_op jit(solution)/shard_map/pallas_call | solution.py:535
  76.4 1.8 %shard_map.68 = (bf16[128,8,512]{2,1,0:T(8,128)(2,1)}, s32[1,1024]{1,0:T(1,128)}, f32[2,2]{1,0:T(2,128)}) custom-call(s32[128,128]{1,0:T(8,128)S(1)} %get-tuple-element.11.spread_ref, bf16[128,8,512]{2,1,0:T(8,128)(2,1)S(1)} %bitcast.7, f32[2,512]{1,0:T(2,128)S(1)} %get-tuple-element.13.affine_ref, s32[1,1024]{1,0:T(1,128)S(1)} %get-tuple-element.14.tally_ref, ...), custom_call_target="tpu_custom_call" | custom-call | tf_op jit(solution)/shard_map/pallas_call | solution.py:607

commit v4 on v3

--- a/solution.py
+++ b/solution.py
@@ -14,7 +14,7 @@
 ROWS = ("rows_0", "rows_1", "rows_2")
 ROWS_REP = ("rows_0", "rows_1", "rows_2", "rep")
 MESH = pl.DeviceIdType.MESH
-LATE = (3, 1)
+LATE = (6, 4)
 BLOCKS = 4
 KERNEL_BYTES = 20 * 2**20
 
@@ -181,7 +181,7 @@
         pltpu.make_async_copy(heard.at[at], heard.at[at], ids_recv.at[at]).wait()
 
     def start_ids(step, carry):
-        ids_copy(plane(step)).start()
+        ids_copy(plane(count_z - step)).start()
         return carry
 
     lax.fori_loop(1, count_z, start_ids, 0)
@@ -312,17 +312,9 @@
     def give(step, carry=0):
         at = plane(step)
 
-        @pl.when(step == 0)
-        def _():
-            pass_on(packed, at)
-
         @pl.when((step >= 1) & jnp.logical_not(is_late(step)))
         def _():
             row_copy(at).start()
-
-        @pl.when(is_late(step))
-        def _():
-            turn(at)
 
         return carry
 
@@ -358,6 +350,9 @@
     ]
     center = jnp.concatenate([jnp.broadcast_to(m, (1, WIDTH)) for m in means], axis=1)
     give(count_z - 1)
+    for step in late_steps:
+        turn(plane(step))
+    pass_on(packed, z)
 
     def squares(at, total):
         used = column[at] >= 0.0

time: 79 us -> 77.6 us (0.982)
  no operation moved by 1% of the time
where the time goes in v4:
time: 77.6 us; the launch traced here: 77.5 us
  Pallas kernels  76.8 us (99%)
    pallas_call x1, Pallas kernels, per_device(): pl.pallas_call(functools.partial(exchange, sizes, slots), out_shape=(jax....  75.1 us
    pallas_call x1, Pallas kernels, per_device(): pl.pallas_call(finished, out_shape=(jax.ShapeDtypeStruct((owners, slots,...  1.76 us

profile of v4, /device:TPU:1, one launch (start us, length us, event | category | flops | bytes accessed | tf_op | source)
XLA Modules:
  0.0 77.5 jit_solution(15078802494606652377)
XLA Ops:
  0.6 75.1 %shard_map.67 = (bf16[4,16,2,8,512]{4,3,2,1,0:T(8,128)(2,1)S(1)}, s32[1,1024]{1,0:T(1,128)S(1)}, f32[2,2]{1,0:T(2,128)S(1)}, f32[2,512]{1,0:T(2,128)S(1)}, s32[128,128]{1,0:T(8,128)S(1)}) custom-call(s32[8,128]{1,0:T(8,128)} %bitcast.8, s32[1,128]{1,0:T(1,128)} %used_hbm.1, f32[1,512]{1,0:T(1,128)} %bitcast.9, bf16[1024,512]{1,0:T(8,128)(2,1)} %table_ref.1), custom_call_target="tpu_custom_call" | custom-call | tf_op jit(solution)/shard_map/pallas_call | solution.py:530
  75.7 1.8 %shard_map.68 = (bf16[128,8,512]{2,1,0:T(8,128)(2,1)}, s32[1,1024]{1,0:T(1,128)}, f32[2,2]{1,0:T(2,128)}) custom-call(s32[128,128]{1,0:T(8,128)S(1)} %get-tuple-element.11.spread_ref, bf16[128,8,512]{2,1,0:T(8,128)(2,1)S(1)} %bitcast.7, f32[2,512]{1,0:T(2,128)S(1)} %get-tuple-element.13.affine_ref, s32[1,1024]{1,0:T(1,128)S(1)} %get-tuple-element.14.tally_ref, ...), custom_call_target="tpu_custom_call" | custom-call | tf_op jit(solution)/shard_map/pallas_call | solution.py:602

commit v5 on v4

--- a/solution.py
+++ b/solution.py
@@ -210,6 +210,16 @@
     totals[...] = jnp.zeros_like(totals)
     tally[...] = jnp.zeros_like(tally)
 
+    def one_hot(wanted):
+        row_of = lax.broadcasted_iota(jnp.int32, wanted.shape, 1).astype(jnp.float32)
+        return jnp.concatenate(
+            [
+                jnp.where(wanted == row_of + float(first), 1.0, 0.0).astype(jnp.bfloat16)
+                for first in range(0, held, LANES)
+            ],
+            axis=1,
+        )
+
     def look(step, carry=0):
         at = plane(step)
         keep_copy(at).wait()
@@ -223,20 +233,10 @@
         wanted = jnp.sum(jnp.where(mine, ids, 0.0), axis=2, keepdims=True)
         wanted = jnp.broadcast_to(wanted, shape).reshape(count_s * slots, LANES)
         column[at] = wanted
-        row_of = lax.broadcasted_iota(jnp.int32, wanted.shape, 1).astype(jnp.float32)
-        hot = jnp.concatenate(
-            [
-                jnp.where(wanted == row_of + float(first), 1.0, 0.0).astype(jnp.bfloat16)
-                for first in range(0, held, LANES)
-            ],
-            axis=1,
-        )
+        hot = one_hot(wanted)
         found = jnp.dot(hot, table[...], preferred_element_type=jnp.float32)
         found = found.reshape(count_s, slots, width)
         packed[at] = found.astype(jnp.bfloat16).reshape(count_x, count_c, slots, width)
-        totals[...] += jnp.sum(found, axis=0)
-        ones = jnp.ones((8, count_s * slots), jnp.bfloat16)
-        tally[...] += jnp.dot(ones, hot, preferred_element_type=jnp.float32)
         return carry
 
     def row_copy(at):
@@ -340,6 +340,19 @@
     lax.fori_loop(1, count_z - 1 - ahead, both, 0)
     lax.fori_loop(count_z - 1 - ahead, count_z, only, 0)
 
+    for step in late_steps:
+        turn(plane(step))
+    give(count_z - 1)
+    pass_on(packed, z)
+
+    def count(at, carry):
+        rows = packed[at].reshape(count_s, slots, width).astype(jnp.float32)
+        totals[...] += jnp.sum(rows, axis=0)
+        ones = jnp.ones((8, count_s * slots), jnp.bfloat16)
+        tally[...] += jnp.dot(ones, one_hot(column[at]), preferred_element_type=jnp.float32)
+        return carry
+
+    lax.fori_loop(0, count_z, count, 0)
     tally_all[y] = tally[0:1].astype(jnp.int32)
     entries = jnp.sum(tally[0:1], axis=1, keepdims=True) * float(WIDTH)
     summed = jnp.sum(totals[...], axis=0, keepdims=True)
@@ -349,10 +362,6 @@
         for layer in range(LAYERS)
     ]
     center = jnp.concatenate([jnp.broadcast_to(m, (1, WIDTH)) for m in means], axis=1)
-    give(count_z - 1)
-    for step in late_steps:
-        turn(plane(step))
-    pass_on(packed, z)
 
     def squares(at, total):
         used = column[at] >= 0.0

time: 77.6 us -> 77.5 us (level)
  no operation moved by 1% of the time
where the time goes in v5:
time: 77.5 us; the launch traced here: 77.2 us
  Pallas kernels  76.6 us (99%)
    pallas_call x1, Pallas kernels, per_device(): pl.pallas_call(functools.partial(exchange, sizes, slots), out_shape=(jax....  74.8 us
    pallas_call x1, Pallas kernels, per_device(): pl.pallas_call(finished, out_shape=(jax.ShapeDtypeStruct((owners, slots,...  1.76 us

profile of v5, /device:TPU:1, one launch (start us, length us, event | category | flops | bytes accessed | tf_op | source)
XLA Modules:
  0.0 77.2 jit_solution(9212829140826082824)
XLA Ops:
  0.6 74.8 %shard_map.67 = (bf16[4,16,2,8,512]{4,3,2,1,0:T(8,128)(2,1)S(1)}, s32[1,1024]{1,0:T(1,128)S(1)}, f32[2,2]{1,0:T(2,128)S(1)}, f32[2,512]{1,0:T(2,128)S(1)}, s32[128,128]{1,0:T(8,128)S(1)}) custom-call(s32[8,128]{1,0:T(8,128)} %bitcast.8, s32[1,128]{1,0:T(1,128)} %used_hbm.1, f32[1,512]{1,0:T(1,128)} %bitcast.9, bf16[1024,512]{1,0:T(8,128)(2,1)} %table_ref.1), custom_call_target="tpu_custom_call" | custom-call | tf_op jit(solution)/shard_map/pallas_call | solution.py:539
  75.5 1.8 %shard_map.68 = (bf16[128,8,512]{2,1,0:T(8,128)(2,1)}, s32[1,1024]{1,0:T(1,128)}, f32[2,2]{1,0:T(2,128)}) custom-call(s32[128,128]{1,0:T(8,128)S(1)} %get-tuple-element.11.spread_ref, bf16[128,8,512]{2,1,0:T(8,128)(2,1)S(1)} %bitcast.7, f32[2,512]{1,0:T(2,128)S(1)} %get-tuple-element.13.affine_ref, s32[1,1024]{1,0:T(1,128)S(1)} %get-tuple-element.14.tally_ref, ...), custom_call_target="tpu_custom_call" | custom-call | tf_op jit(solution)/shard_map/pallas_call | solution.py:611
